TPU v7x, 32 devices: a whole 2x2x4 slice. The times are simulated.
32 devices in a mesh: grp: 4 (over y, x), dev: 8 (over z, core).
Axes of the slice: x: 2, y: 2, z: 4, core: 2. Of those that a mesh axis runs over, the one named last changes fastest.
Arguments:
- token_ids: int32 [128, 128], P(('grp', 'dev')), may hold values from 0 to 128255, as said below
- sensitivity: bfloat16 [128, 128, 4096], P(('grp', 'dev')), may hold values from -6 to 6
- last_hidden: bfloat16 [128, 4096], P(('grp', 'dev')), may hold values from -6 to 6
- lengths: int32 [128], P(('grp', 'dev')), may hold values from 97 to 128
- norm_gain: float32 [4096], replicated, may hold values from 0.25 to 1.75
- reward_head: float32 [4096], replicated, may hold values from -0.09375 to 0.09375
- chosen_index: int32 [64], replicated, may hold values from 0 to 127, as said below
- rejected_index: int32 [64], replicated, may hold values from 0 to 127, as said below
- shard_owner: int32 [32], replicated, may hold values from 0 to 31, each once
Outputs:
- owned_grad: bfloat16 [128256, 4096], P(('grp', 'dev'))
- head_grad: float32 [4096], P(('grp', 'dev'))
Inputs may be any that keep to these rules, and one draw needn't show every extreme that they name: `token_ids`: within the token slots of one device, at most 32 ids fall in any one vocabulary shard of 4008 rows, and on every device some shard gets exactly 32. chosen_index and rejected_index together name every response exactly once. `rejected_index`: see chosen_index.
All inputs are finite; a program needn't handle non-finite values.
Results may differ from a plain program's by a relative error of at most 0.0042.
Values may be sent and summed in bfloat16 or wider, within the bound.
A program may use at most 128 MiB of HBM per device.

v0:
```python
import jax
import jax.numpy as jnp
from jax import lax
from jax.sharding import PartitionSpec as P

VOCAB = 128256


def local(
    token_ids,
    sensitivity,
    last_hidden,
    lengths,
    norm_gain,
    reward_head,
    chosen_index,
    rejected_index,
    shard_owner,
):
    resp_local, block_len = token_ids.shape
    width = sensitivity.shape[2]
    tok_local = resp_local * block_len
    n_grp = lax.axis_size("grp")
    n_dev = lax.axis_size("dev")
    devices = shard_owner.shape[0]
    shard_rows = VOCAB // devices
    capacity = max(2, (2 * tok_local + devices - 1) // devices)
    hidden = last_hidden.astype(jnp.float32)
    normed = (
        hidden / jnp.sqrt(jnp.mean(hidden * hidden, axis=-1, keepdims=True) + 1e-05) * norm_gain
    )
    own_reward = jnp.sum(normed * reward_head, axis=-1)
    reward = lax.all_gather(own_reward, ("grp", "dev"), axis=0, tiled=True)
    margin = reward[chosen_index] - reward[rejected_index]
    push = -jax.nn.sigmoid(-margin)
    mine = lax.axis_index(("grp", "dev")) * resp_local + jnp.arange(resp_local, dtype=jnp.int32)
    sign_table = (chosen_index[None, :] == mine[:, None]).astype(jnp.float32) - (
        rejected_index[None, :] == mine[:, None]
    ).astype(jnp.float32)
    reward_grad = jnp.sum(sign_table * push[None, :], axis=1)
    head_grad = lax.psum_scatter(
        jnp.sum(reward_grad[:, None] * normed, axis=0),
        ("grp", "dev"),
        scatter_dimension=0,
        tiled=True,
    )
    positions = jnp.arange(block_len, dtype=jnp.int32)
    scale = jnp.where(positions[None, :] < lengths[:, None], reward_grad[:, None], jnp.float32(0.0))
    grad_rows = (scale[:, :, None] * sensitivity).astype(jnp.bfloat16).reshape(tok_local, width)
    ids = token_ids.reshape(tok_local)
    shard_of = ids // shard_rows
    offset = ids - shard_of * shard_rows
    owner = shard_owner[shard_of]
    owner_hot = (owner[:, None] == jnp.arange(devices, dtype=jnp.int32)[None, :]).astype(
        jnp.bfloat16
    )
    token_pos = jnp.arange(tok_local, dtype=jnp.int32)
    earlier = (token_pos[:, None] > token_pos[None, :]).astype(jnp.bfloat16)
    before = jnp.dot(earlier, owner_hot, preferred_element_type=jnp.float32)
    rank = jnp.sum(before * owner_hot.astype(jnp.float32), axis=1).astype(jnp.int32)
    slot = owner * capacity + rank
    slot_match = slot[None, :] == jnp.arange(devices * capacity, dtype=jnp.int32)[:, None]
    outgoing = jnp.dot(
        slot_match.astype(jnp.bfloat16), grad_rows, preferred_element_type=jnp.float32
    ).astype(jnp.bfloat16)
    outgoing = outgoing.reshape(n_grp, n_dev, capacity, width)
    targets = jnp.sum(jnp.where(slot_match, offset[None, :] + 1, 0), axis=1) - 1
    targets = targets.reshape(n_grp, n_dev, capacity)
    arrived, arrived_rows = (
        lax.all_to_all(
            lax.all_to_all(outgoing, "grp", split_axis=0, concat_axis=0, tiled=True),
            "dev",
            split_axis=1,
            concat_axis=1,
            tiled=True,
        ),
        lax.all_to_all(
            lax.all_to_all(targets, "grp", split_axis=0, concat_axis=0, tiled=True),
            "dev",
            split_axis=1,
            concat_axis=1,
            tiled=True,
        ),
    )
    arrived = arrived.reshape(devices * capacity, width)
    arrived_rows = arrived_rows.reshape(devices * capacity)
    placing = (arrived_rows[None, :] == jnp.arange(shard_rows, dtype=jnp.int32)[:, None]).astype(
        jnp.bfloat16
    )
    owned = jnp.dot(placing, arrived, preferred_element_type=jnp.float32).astype(jnp.bfloat16)
    return (owned, head_grad)


def solution(mesh):
    placed = (
        P(("grp", "dev"), None),
        P(("grp", "dev"), None, None),
        P(("grp", "dev"), None),
        P(("grp", "dev")),
        P(),
        P(),
        P(),
        P(),
        P(),
    )
    return jax.shard_map(
        local,
        mesh=mesh,
        in_specs=placed,
        out_specs=(P(("grp", "dev"), None), P(("grp", "dev"))),
        check_vma=False,
    )
```

profile of v0, /device:TPU:11, one launch (start us, length us, event | category | flops | bytes accessed | tf_op | source)
XLA Modules:
  0.0 455.7 jit_solution(17698760418846959356)
XLA Ops:
  0.6 0.7 fusion.13
  1.3 0.7 broadcast_divide_fusion
  2.0 1.8 fusion.16
  3.8 2.1 fusion.15
  5.9 4.3 compare_select_fusion.1
  10.3 0.2 compare_reduce_fusion.24
  10.4 15.8 %select_select_fusion = s32[512]{0:T(512)S(1)} fusion(pred[512]{0:T(512)(128)(4,1)S(1)} %get-tuple-element.26, pred[512]{0:T(512)(128)(4,1)S(1)} %get-tuple-element.25, pred[512]{0:T(512)(128)(4,1)S(1)} %get-tuple-element.24, pred[512]{0:T(512)(128)(4,1)S(1)} %get-tuple-element.23, pred[512]{0:T(512)(128)(4,1)S(1)} %get-tuple-element.22, ...), kind=kLoop, calls=%fused_computation.66 | loop fusion | flops 12800 | bytes 16996 | tf_op jit(solution)/shard_map/gather | solution.py:53
  26.2 0.3 fusion.1
  26.5 0.7 fusion.9
  27.2 0.3 select_reduce_fusion
  27.5 0.1 sub.35
  27.6 0.7 reshape.343
  28.2 3.7 all-to-all-start
  31.9 0.9 fusion.4
  32.9 0.7 compare_select_fusion.8
  33.5 0.7 compare_select_fusion.7
  34.2 1.0 multiply_reduce_fusion.1
  35.2 0.2 dynamic-update-slice
  35.5 40.0 %all-reduce = f32[128]{0:T(128)S(1)} all-reduce(f32[128]{0:T(128)S(1)} %dynamic-update-slice), channel_id=1, replica_groups=mesh['grp'=4,'dev'=8] {'grp','dev'}, use_global_device_ids=true, to_apply=%add | all-reduce | flops 128 | bytes 1024
  75.4 0.8 gather_fusion
  76.2 0.8 gather_fusion.1
  77.0 0.9 multiply_reduce_fusion.2
  77.9 0.7 fusion.11
  78.6 3.7 multiply_convert_fusion
  82.3 6.8 %convolution_convert_fusion.1 = bf16[1024,4096]{1,0:T(8,128)(2,1)} fusion(bf16[512,4096]{1,0:T(8,128)(2,1)S(1)} %bitcast.73, s32[512]{0:T(512)S(1)} %get-tuple-element.64), kind=kOutput, calls=%fused_computation.6 | convolution fusion | flops 4299685888 | bytes 12584960 | tf_op jit(solution)/shard_map/dot_general | solution.py:63
  89.1 0.0 all-to-all-done
  89.1 6.0 %all-to-all-start.2 = ((bf16[4,8,32,4096]{3,2,1,0:T(8,128)(2,1)}), bf16[4,8,32,4096]{3,2,1,0:T(8,128)(2,1)}, u32[]{:S(2)}, u32[]{:S(2)}) async-start(bf16[4,8,32,4096]{3,2,1,0:T(8,128)(2,1)} %bitcast.71), calls=%async_computation.2 | async-start | bytes 16777216 | tf_op jit(solution)/shard_map/all_to_all | solution.py:71
  95.1 0.5 broadcast.444
  95.6 0.6 reduce.50
  96.3 0.1 reshape.344
  96.4 0.7 reshape.345
  97.0 88.5 %all-to-all-done.2 = bf16[4,8,32,4096]{3,2,1,0:T(8,128)(2,1)} async-done(((bf16[4,8,32,4096]{3,2,1,0:T(8,128)(2,1)}), bf16[4,8,32,4096]{3,2,1,0:T(8,128)(2,1)}, u32[]{:S(2)}, u32[]{:S(2)}) %all-to-all-start.2) | async-done | bytes 8388640 | tf_op jit(solution)/shard_map/all_to_all | solution.py:71
  185.6 6.3 %all-to-all-start.1 = ((s32[8,1,128]{2,1,0:T(1,128)}), s32[8,1,128]{2,1,0:T(1,128)S(1)}, u32[]{:S(2)}, u32[]{:S(2)}) async-start(s32[8,1,128]{2,1,0:T(1,128)} %reshape.345), calls=%async_computation.1 | async-start | bytes 8192 | tf_op jit(solution)/shard_map/all_to_all | solution.py:77
  191.9 7.9 %copy.22 = bf16[4,8,32,4096]{3,2,0,1:T(8,128)(2,1)} copy(bf16[4,8,32,4096]{3,2,1,0:T(8,128)(2,1)} %all-to-all-done.2) | data formatting | bytes 16777216 | tf_op jit(solution)/shard_map/all_to_all | solution.py:71
  199.8 0.0 all-to-all-done.1
  199.8 5.1 %all-to-all-start.3 = ((bf16[4,8,32,4096]{3,2,0,1:T(8,128)(2,1)}), bf16[4,8,32,4096]{3,2,0,1:T(8,128)(2,1)}, u32[]{:S(2)}, u32[]{:S(2)}) async-start(bf16[4,8,32,4096]{3,2,0,1:T(8,128)(2,1)} %copy.22), calls=%async_computation.3 | async-start | bytes 16777216 | tf_op jit(solution)/shard_map/all_to_all | solution.py:70
  204.9 0.1 multiply_reduce_fusion
  205.0 200.8 %all-reduce.1 = f32[4096]{0:T(1024)S(1)} all-reduce(f32[4096]{0:T(1024)S(1)} %multiply_reduce_fusion), channel_id=2, replica_groups=mesh['grp'=4,'dev'=8] {'grp','dev'}, use_global_device_ids=true, to_apply=%region_6.7.clone | all-reduce | flops 4096 | bytes 32768
  405.7 0.6 dynamic-slice
  406.3 0.6 reduce.51
  407.0 0.1 reshape.346
  407.1 0.1 eq.71
  407.1 0.0 all-to-all-done.3
  407.1 7.7 %copy.23 = bf16[4,8,32,4096]{3,2,1,0:T(8,128)(2,1)} copy(bf16[4,8,32,4096]{3,2,0,1:T(8,128)(2,1)} %all-to-all-done.3) | data formatting | bytes 16777216 | tf_op jit(solution)/shard_map/all_to_all | solution.py:70
  414.8 40.8 %convolution_convert_fusion = bf16[4008,4096]{1,0:T(8,128)(2,1)} fusion(bf16[1024,4096]{1,0:T(8,128)(2,1)} %bitcast.72, s32[1024]{0:T(1024)S(1)} %eq.71), kind=kOutput, calls=%fused_computation.2 | convolution fusion | flops 33642061824 | bytes 41226240 | tf_op jit(solution)/shard_map/dot_general | solution.py:90
  (9 shorter events, 0.1 us)
Async XLA Ops:
  28.2 60.9 %all-to-all-start = ((s32[4,1,256]{2,1,0:T(1,128)}), s32[4,1,256]{2,1,0:T(1,128)S(1)}, u32[]{:S(2)}, u32[]{:S(2)}) async-start(s32[4,1,256]{2,1,0:T(1,128)} %reshape.343), calls=%async_computation | async-start | bytes 8192 | tf_op jit(solution)/shard_map/all_to_all | solution.py:78
  89.1 96.4 %all-to-all-start.2 = ((bf16[4,8,32,4096]{3,2,1,0:T(8,128)(2,1)}), bf16[4,8,32,4096]{3,2,1,0:T(8,128)(2,1)}, u32[]{:S(2)}, u32[]{:S(2)}) async-start(bf16[4,8,32,4096]{3,2,1,0:T(8,128)(2,1)} %bitcast.71), calls=%async_computation.2 | async-start | bytes 16777216 | tf_op jit(solution)/shard_map/all_to_all | solution.py:71
  185.6 14.2 %all-to-all-start.1 = ((s32[8,1,128]{2,1,0:T(1,128)}), s32[8,1,128]{2,1,0:T(1,128)S(1)}, u32[]{:S(2)}, u32[]{:S(2)}) async-start(s32[8,1,128]{2,1,0:T(1,128)} %reshape.345), calls=%async_computation.1 | async-start | bytes 8192 | tf_op jit(solution)/shard_map/all_to_all | solution.py:77
  199.8 207.4 %all-to-all-start.3 = ((bf16[4,8,32,4096]{3,2,0,1:T(8,128)(2,1)}), bf16[4,8,32,4096]{3,2,0,1:T(8,128)(2,1)}, u32[]{:S(2)}, u32[]{:S(2)}) async-start(bf16[4,8,32,4096]{3,2,0,1:T(8,128)(2,1)} %copy.22), calls=%async_computation.3 | async-start | bytes 16777216 | tf_op jit(solution)/shard_map/all_to_all | solution.py:70
where the time goes:
time: 460 us; the launch traced here: 456 us
  blocking collectives  241 us (52%)
  waiting for transfers between devices  88.5 us (19%)
  matrix products  47.9 us (10%)
  other arithmetic  32.6 us (7%)
  local copies, waits for them, and re-layouts  24.1 us (5%)
  starting transfers between devices  21.1 us (5%)
    unnamed x2, blocking collectives  241 us
    all_to_all x1, waiting for transfers between devices, local(): lax.all_to_all(outgoing, 'grp', split_axis=0, concat_axis=0, tiled=True)  88.5 us
    dot_general x1, matrix products, local(): jnp.dot(placing, arrived, preferred_element_type=jnp.float32)  40.8 us
    gather x3, other arithmetic, local(): owner = shard_owner[shard_of]  20.3 us
  transfers between devices with their start and end apart: 4, of which 1 were waited for; matrix products, arithmetic and copies ran while one was open for 6% of the time, Pallas kernels for 0%

commit v1 on v0

v1 whole, which is shorter than its diff:
```python
import functools

import jax
import jax.numpy as jnp
from jax import lax
from jax.experimental import pallas as pl
from jax.experimental.pallas import tpu as pltpu
from jax.sharding import PartitionSpec as P

VOCAB = 128256
MESH = pl.DeviceIdType.MESH


def exchange_kernel(n, n_dev, meta_ref, rows_ref, meta_out, rows_out, send_sem, recv_sem, own_sem):
    me = lax.axis_index("grp") * n_dev + lax.axis_index("dev")

    def coord(t):
        return (t // n_dev, lax.rem(t, n_dev))

    barrier = pltpu.get_barrier_semaphore()

    def greet(k, c):
        t = lax.rem(me + k, n)
        pl.semaphore_signal(barrier, inc=1, device_id=coord(t), device_id_type=MESH)
        return c

    lax.fori_loop(1, n, greet, 0)
    own = [
        pltpu.make_async_copy(src.at[me], dst.at[me], own_sem.at[i])
        for i, (src, dst) in enumerate(((meta_ref, meta_out), (rows_ref, rows_out)))
    ]
    for c in own:
        c.start()
    pl.semaphore_wait(barrier, n - 1)

    def copies(src_block, dst_block, to):
        return [
            pltpu.make_async_remote_copy(
                src_ref=src.at[src_block],
                dst_ref=dst.at[dst_block],
                send_sem=send_sem.at[i, src_block],
                recv_sem=recv_sem.at[i, dst_block],
                device_id=coord(to),
                device_id_type=MESH,
            )
            for i, (src, dst) in enumerate(((meta_ref, meta_out), (rows_ref, rows_out)))
        ]

    def send(k, c):
        t = lax.rem(me + k, n)
        for cp in copies(t, me, t):
            cp.start()
        return c

    lax.fori_loop(1, n, send, 0)

    def finish(k, c):
        t = lax.rem(me + k, n)
        for cp in copies(t, me, t):
            cp.wait_send()
        s = lax.rem(me + n - k, n)
        for cp in copies(s, s, s):
            cp.wait_recv()
        return c

    lax.fori_loop(1, n, finish, 0)
    for c in own:
        c.wait()


def exchange(meta, rows, n, n_dev):
    anyspec = pl.BlockSpec(memory_space=pl.ANY)
    return pl.pallas_call(
        functools.partial(exchange_kernel, n, n_dev),
        out_shape=(
            jax.ShapeDtypeStruct(meta.shape, meta.dtype),
            jax.ShapeDtypeStruct(rows.shape, rows.dtype),
        ),
        in_specs=[anyspec, anyspec],
        out_specs=(anyspec, anyspec),
        scratch_shapes=[
            pltpu.SemaphoreType.DMA((2, n)),
            pltpu.SemaphoreType.DMA((2, n)),
            pltpu.SemaphoreType.DMA((2,)),
        ],
        compiler_params=pltpu.CompilerParams(collective_id=0, has_side_effects=True),
    )(meta, rows)


def local(
    token_ids,
    sensitivity,
    last_hidden,
    lengths,
    norm_gain,
    reward_head,
    chosen_index,
    rejected_index,
    shard_owner,
):
    resp_local, block_len = token_ids.shape
    width = sensitivity.shape[2]
    tok_local = resp_local * block_len
    n_dev = lax.axis_size("dev")
    devices = shard_owner.shape[0]
    responses = devices * resp_local
    shard_rows = VOCAB // devices
    capacity = max(2, (2 * tok_local + devices - 1) // devices)
    cols = width // devices
    lanes = -(-max(cols, capacity, resp_local) // 128) * 128
    hidden = last_hidden.astype(jnp.float32)
    normed = (
        hidden / jnp.sqrt(jnp.mean(hidden * hidden, axis=-1, keepdims=True) + 1e-05) * norm_gain
    )
    own_reward = jnp.sum(normed * reward_head, axis=-1)

    positions = jnp.arange(block_len, dtype=jnp.int32)
    live = (positions[None, :] < lengths[:, None]).reshape(tok_local)
    ids = token_ids.reshape(tok_local)
    shard_of = ids // shard_rows
    offset = ids - shard_of * shard_rows
    shard_hot = shard_of[:, None] == jnp.arange(devices, dtype=jnp.int32)[None, :]
    owner = jnp.sum(jnp.where(shard_hot, shard_owner[None, :], 0), axis=1)
    live_hot = (shard_hot & live[:, None]).astype(jnp.bfloat16)
    token_pos = jnp.arange(tok_local, dtype=jnp.int32)
    earlier = (token_pos[:, None] > token_pos[None, :]).astype(jnp.bfloat16)
    before = jnp.dot(earlier, live_hot, preferred_element_type=jnp.float32)
    rank = jnp.sum(before * live_hot.astype(jnp.float32), axis=1).astype(jnp.int32)
    slot = jnp.where(live, owner * capacity + rank, -1)
    slot_match = slot[None, :] == jnp.arange(devices * capacity, dtype=jnp.int32)[:, None]
    outgoing = jnp.dot(
        slot_match.astype(jnp.bfloat16),
        sensitivity.reshape(tok_local, width),
        preferred_element_type=jnp.float32,
    ).astype(jnp.bfloat16)
    code = (offset + 1) * resp_local + token_pos // block_len
    codes = jnp.sum(jnp.where(slot_match, code[None, :], 0), axis=1)
    codes = codes.reshape(devices, capacity)
    target_out = codes // resp_local - 1
    resp_out = codes - codes // resp_local * resp_local

    def lane_pad(a):
        return jnp.pad(a, ((0, 0), (0, lanes - a.shape[1])))[:, None, :]

    normed_blocks = normed.reshape(resp_local, devices, cols).transpose(1, 0, 2)
    meta = jnp.concatenate(
        [
            lane_pad(target_out.astype(jnp.float32)),
            lane_pad(resp_out.astype(jnp.float32)),
            lane_pad(jnp.broadcast_to(own_reward[None, :], (devices, resp_local))),
            jnp.zeros((devices, 1, lanes), jnp.float32),
            jnp.pad(normed_blocks, ((0, 0), (0, 0), (0, lanes - cols))),
        ],
        axis=1,
    )
    extra = -meta.shape[1] % 8
    meta = jnp.pad(meta, ((0, 0), (0, extra), (0, 0)))
    meta_in, arrived = exchange(
        meta, outgoing.reshape(devices, capacity, width), devices, n_dev
    )

    targets = meta_in[:, 0, :capacity].astype(jnp.int32).reshape(devices * capacity)
    resp_in = meta_in[:, 1, :capacity].astype(jnp.int32)
    reward = meta_in[:, 2, :resp_local].reshape(responses)
    normed_in = meta_in[:, 4 : 4 + resp_local, :cols]
    all_resp = jnp.arange(responses, dtype=jnp.int32)
    sign_table = (chosen_index[:, None] == all_resp[None, :]).astype(jnp.float32) - (
        rejected_index[:, None] == all_resp[None, :]
    ).astype(jnp.float32)
    margin = jnp.sum(sign_table * reward[None, :], axis=1)
    push = -jax.nn.sigmoid(-margin)
    reward_grad = jnp.sum(sign_table * push[:, None], axis=0).reshape(devices, resp_local)
    head_grad = jnp.sum(reward_grad[:, :, None] * normed_in, axis=(0, 1))
    resp_hot = resp_in[:, :, None] == jnp.arange(resp_local, dtype=jnp.int32)[None, None, :]
    scale = jnp.sum(jnp.where(resp_hot, reward_grad[:, None, :], 0.0), axis=2)
    scaled = (scale[:, :, None] * arrived).astype(jnp.bfloat16).reshape(devices * capacity, width)
    placing = (targets[None, :] == jnp.arange(shard_rows, dtype=jnp.int32)[:, None]).astype(
        jnp.bfloat16
    )
    owned = jnp.dot(placing, scaled, preferred_element_type=jnp.float32).astype(jnp.bfloat16)
    return (owned, head_grad)


def solution(mesh):
    placed = (
        P(("grp", "dev"), None),
        P(("grp", "dev"), None, None),
        P(("grp", "dev"), None),
        P(("grp", "dev")),
        P(),
        P(),
        P(),
        P(),
        P(),
    )
    return jax.shard_map(
        local,
        mesh=mesh,
        in_specs=placed,
        out_specs=(P(("grp", "dev"), None), P(("grp", "dev"))),
        check_vma=False,
    )
```

time: 460 us -> 270 us (0.59)
  blocking collectives: 241 us -> 0 us
  Pallas kernels: 0 us -> 198 us
  waiting for transfers between devices: 88.5 us -> 0 us
  local copies, waits for them, and re-layouts: 24.1 us -> 2.2 us
  starting transfers between devices: 21.1 us -> 0 us
  other arithmetic: 32.6 us -> 18.9 us
    unnamed x2 -> x0, blocking collectives: 241 us -> none
    pallas_call x0 -> x1, Pallas kernels: none -> 198 us  [exchange(): pl.pallas_call(functools.partial(exchange_kernel, n, n_dev), out_shape=(j...]
    all_to_all x4 -> x0, waiting for transfers between devices: 88.5 us -> none  [the longest x1 88.5 us: local(): lax.all_to_all(outgoing, 'grp', split_axis=0, concat_axis=0, tiled=True)]
    all_to_all x4 -> x0, starting transfers between devices: 21.1 us -> none  [the longest x1 6.33 us: local(): lax.all_to_all(lax.all_to_all(targets, 'grp', split_axis=0, concat_axis=0...]
    gather x5 -> x0, other arithmetic: 20.3 us -> none  [the longest x3 20.3 us: local(): owner = shard_owner[shard_of]]
    all_to_all x5 -> x0, local copies, waits for them, and re-layouts: 16.1 us -> none  [the longest x1 7.89 us: local(): lax.all_to_all(outgoing, 'grp', split_axis=0, concat_axis=0, tiled=True)]
    convert_element_type x1 -> x4, other arithmetic: 3.71 us -> 11.9 us  [the longest x1 9.98 us: local(): (scale[:, :, None] * arrived).astype(jnp.bfloat16)]
    gather x4 -> x0, local copies, waits for them, and re-layouts: 5.47 us -> none  [the longest x2 3.91 us: local(): owner = shard_owner[shard_of]]
  transfers between devices with their start and end apart: 4 -> 0, of which waited for: 1 -> 0; matrix products, arithmetic and copies ran while one was open for 6% -> 0% of each run, Pallas kernels for 0% -> 0%
where the time goes in v1:
time: 270 us; the launch traced here: 269 us
  Pallas kernels  198 us (73%)
  matrix products  50 us (19%)
  other arithmetic  18.9 us (7%)
    pallas_call x1, Pallas kernels, exchange(): pl.pallas_call(functools.partial(exchange_kernel, n, n_dev), out_shape=(j...  198 us
    dot_general x1, matrix products, local(): jnp.dot(placing, scaled, preferred_element_type=jnp.float32)  40.8 us
    convert_element_type x1, other arithmetic, local(): (scale[:, :, None] * arrived).astype(jnp.bfloat16)  9.98 us
    dot_general x1, matrix products, local(): jnp.dot(slot_match.astype(jnp.bfloat16), sensitivity.reshape(tok_local, w...  8.88 us

profile of v1, /device:TPU:11, one launch (start us, length us, event | category | flops | bytes accessed | tf_op | source)
XLA Modules:
  0.0 269.3 jit_solution(1641995160583314315)
XLA Ops:
  0.6 0.9 fusion.4
  1.5 0.7 fusion.20
  2.3 0.7 add_select_fusion.2
  3.0 0.3 fusion.1
  3.3 0.7 select_reduce_fusion.2
  4.0 0.7 add_select_fusion.3
  4.7 0.3 select_reduce_fusion
  5.0 0.1 reshape.151
  5.1 1.0 fusion.22
  6.2 0.8 concatenate.3.meta_ref
  6.9 8.9 %convolution_convert_fusion.1 = bf16[1024,4096]{1,0:T(8,128)(2,1)} fusion(bf16[512,4096]{1,0:T(8,128)(2,1)} %bitcast.46, s32[512]{0:T(512)S(1)} %add_select_fusion.3), kind=kOutput, calls=%fused_computation.4 | convolution fusion | flops 4299685888 | bytes 12584960 | tf_op jit(solution)/shard_map/dot_general | solution.py:131
  15.8 0.0 copy-start
  15.8 0.0 copy-start.1
  15.8 197.5 %shard_map.104 = (f32[32,8,128]{2,1,0:T(8,128)}, bf16[32,32,4096]{2,1,0:T(8,128)(2,1)}) custom-call(f32[32,8,128]{2,1,0:T(8,128)} %concatenate.3.meta_ref, bf16[32,32,4096]{2,1,0:T(8,128)(2,1)} %bitcast.42), custom_call_target="tpu_custom_call" | custom-call | tf_op jit(solution)/shard_map/pallas_call | solution.py:73
  213.3 1.0 slice_reduce_fusion
  214.3 0.1 mul.100
  214.4 0.0 copy-done
  214.4 0.0 copy-done.1
  214.4 0.2 multiply_reduce_fusion.3
  214.6 0.1 multiply_reduce_fusion.2
  214.7 0.1 broadcast_in_dim.86
  214.9 1.5 multiply_reduce_fusion
  216.4 0.1 copy.14
  216.5 0.9 slice_convert_fusion
  217.4 1.0 convert_reduce_fusion
  218.4 0.1 convert_element_type.76
  218.4 0.1 select_reduce_fusion.1
  218.5 10.0 %multiply_convert_fusion = bf16[32,32,4096]{2,1,0:T(8,128)(2,1)} fusion(bf16[32,32,4096]{2,1,0:T(8,128)(2,1)} %get-tuple-element.5, f32[32,32]{1,0:T(8,128)S(1)} %select_reduce_fusion.1), kind=kLoop, calls=%fused_computation.1 | loop fusion | flops 12582912 | bytes 16781312 | tf_op jit(solution)/shard_map/convert_element_type | solution.py:176
  228.5 40.8 %convolution_convert_fusion = bf16[4008,4096]{1,0:T(8,128)(2,1)} fusion(bf16[1024,4096]{1,0:T(8,128)(2,1)} %bitcast.41, s32[1024]{0:T(1024)S(1)} %convert_element_type.76), kind=kOutput, calls=%fused_computation | convolution fusion | flops 33642061824 | bytes 41226240 | tf_op jit(solution)/shard_map/dot_general | solution.py:180
  (8 shorter events, 0.1 us)
Async XLA Ops:
  15.8 198.6 %copy-start = (s32[64]{0:T(128)S(1)}, s32[64]{0:T(128)}, u32[]{:S(2)}) copy-start(s32[64]{0:T(128)} %param.16) | copy-start | bytes 772
  15.8 198.6 %copy-start.1 = (s32[64]{0:T(128)S(1)}, s32[64]{0:T(128)}, u32[]{:S(2)}) copy-start(s32[64]{0:T(128)} %param.15) | copy-start | bytes 772

commit v2 on v1

--- a/solution.py
+++ b/solution.py
@@ -173,11 +173,54 @@
     head_grad = jnp.sum(reward_grad[:, :, None] * normed_in, axis=(0, 1))
     resp_hot = resp_in[:, :, None] == jnp.arange(resp_local, dtype=jnp.int32)[None, None, :]
     scale = jnp.sum(jnp.where(resp_hot, reward_grad[:, None, :], 0.0), axis=2)
-    scaled = (scale[:, :, None] * arrived).astype(jnp.bfloat16).reshape(devices * capacity, width)
-    placing = (targets[None, :] == jnp.arange(shard_rows, dtype=jnp.int32)[:, None]).astype(
-        jnp.bfloat16
-    )
-    owned = jnp.dot(placing, scaled, preferred_element_type=jnp.float32).astype(jnp.bfloat16)
+    total = devices * capacity
+    scale = scale.reshape(total)
+    rows_in = arrived.reshape(total, width)
+
+    def place_all(operands):
+        rows, targets, scale = operands
+        scaled = (scale[:, None] * rows).astype(jnp.bfloat16)
+        placing = (targets[None, :] == jnp.arange(shard_rows, dtype=jnp.int32)[:, None]).astype(
+            jnp.bfloat16
+        )
+        return jnp.dot(placing, scaled, preferred_element_type=jnp.float32).astype(jnp.bfloat16)
+
+    operands = (rows_in, targets, scale)
+    blocks, window = 3, total // 4
+    if shard_rows % (8 * blocks) or window % 128:
+        owned = place_all(operands)
+        return (owned, head_grad)
+    block_rows = shard_rows // blocks
+    first_row = jnp.arange(blocks, dtype=jnp.int32) * block_rows
+    in_block = (targets[:, None] >= first_row[None, :]) & (
+        targets[:, None] < first_row[None, :] + block_rows
+    )
+    block_hot = in_block.astype(jnp.bfloat16)
+    pos = jnp.arange(total, dtype=jnp.int32)
+    ahead = (pos[:, None] > pos[None, :]).astype(jnp.bfloat16)
+    rank_in = jnp.dot(ahead, block_hot, preferred_element_type=jnp.float32).astype(jnp.int32)
+    slot_base = jnp.arange(blocks, dtype=jnp.int32) * window
+    packed_slot = jnp.sum(jnp.where(in_block, rank_in + slot_base[None, :] + 1, 0), axis=1) - 1
+    fits = jnp.max(jnp.sum(in_block.astype(jnp.int32), axis=0)) <= window
+
+    def place_packed(operands):
+        rows, targets, scale = operands
+        pack = packed_slot[None, :] == jnp.arange(blocks * window, dtype=jnp.int32)[:, None]
+        packed_scale = jnp.sum(jnp.where(pack, scale[None, :], 0.0), axis=1)
+        packed_target = jnp.sum(jnp.where(pack, targets[None, :] + 1, 0), axis=1) - 1
+        packed = jnp.dot(pack.astype(jnp.bfloat16), rows, preferred_element_type=jnp.float32)
+        packed = (packed_scale[:, None] * packed).astype(jnp.bfloat16)
+        row_of = first_row[:, None] + jnp.arange(block_rows, dtype=jnp.int32)[None, :]
+        placing = packed_target.reshape(blocks, 1, window) == row_of[:, :, None]
+        owned = lax.dot_general(
+            placing.astype(jnp.bfloat16),
+            packed.reshape(blocks, window, width),
+            (((2,), (1,)), ((0,), (0,))),
+            preferred_element_type=jnp.float32,
+        )
+        return owned.astype(jnp.bfloat16).reshape(shard_rows, width)
+
+    owned = lax.cond(fits, place_packed, place_all, operands)
     return (owned, head_grad)
 
 

time: 270 us -> 252 us (0.933)
  matrix products: 50 us -> 39 us
  other arithmetic: 18.9 us -> 10.8 us
    dot_general x1 -> x3, matrix products: 40.8 us -> 29.9 us  [the longest x1 17.4 us: place_packed(): lax.dot_general(placing.astype(jnp.bfloat16), packed.reshape(blocks, wind...]
    convert_element_type x1 -> x0, other arithmetic: 9.98 us -> none  [local(): (scale[:, :, None] * arrived).astype(jnp.bfloat16)]
where the time goes in v2:
time: 252 us; the launch traced here: 251 us
  Pallas kernels  198 us (79%)
  matrix products  39 us (15%)
  other arithmetic  10.8 us (4%)
    pallas_call x1, Pallas kernels, exchange(): pl.pallas_call(functools.partial(exchange_kernel, n, n_dev), out_shape=(j...  198 us
    dot_general x1, matrix products, place_packed(): lax.dot_general(placing.astype(jnp.bfloat16), packed.reshape(blocks, wind...  17.4 us
    dot_general x1, matrix products, place_packed(): jnp.dot(pack.astype(jnp.bfloat16), rows, preferred_element_type=jnp.float32)  12 us
    dot_general x1, matrix products, local(): jnp.dot(slot_match.astype(jnp.bfloat16), sensitivity.reshape(tok_local, w...  8.89 us

profile of v2, /device:TPU:11, one launch (start us, length us, event | category | flops | bytes accessed | tf_op | source)
XLA Modules:
  0.0 251.3 jit_solution(8812491330006134046)
XLA Ops:
  0.6 0.9 fusion.11
  1.5 0.7 fusion.27
  2.3 0.7 add_select_fusion.2
  3.0 0.3 fusion.7
  3.3 0.7 select_reduce_fusion.5
  4.0 0.7 add_select_fusion.3
  4.7 0.3 select_reduce_fusion.3
  5.0 0.1 reshape.209
  5.2 1.0 fusion.30
  6.2 0.8 concatenate.3.meta_ref
  7.0 8.9 %convolution_convert_fusion.2 = bf16[1024,4096]{1,0:T(8,128)(2,1)} fusion(bf16[512,4096]{1,0:T(8,128)(2,1)} %bitcast.57, s32[512]{0:T(512)S(1)} %add_select_fusion.3), kind=kOutput, calls=%fused_computation.21 | convolution fusion | flops 4299685888 | bytes 12584960 | tf_op jit(solution)/shard_map/dot_general | solution.py:131
  15.8 0.0 copy-start
  15.8 0.0 copy-start.1
  15.8 197.5 %shard_map.104 = (f32[32,8,128]{2,1,0:T(8,128)}, bf16[32,32,4096]{2,1,0:T(8,128)(2,1)}) custom-call(f32[32,8,128]{2,1,0:T(8,128)} %concatenate.3.meta_ref, bf16[32,32,4096]{2,1,0:T(8,128)(2,1)} %bitcast.48), custom_call_target="tpu_custom_call" | custom-call | tf_op jit(solution)/shard_map/pallas_call | solution.py:73
  213.4 1.0 slice_reduce_fusion
  214.3 0.1 mul.131
  214.4 0.0 copy-done
  214.4 0.0 copy-done.1
  214.4 0.2 multiply_reduce_fusion.3
  214.6 0.1 multiply_reduce_fusion.2
  214.8 0.1 broadcast_in_dim.127
  214.9 1.5 multiply_reduce_fusion
  216.4 0.1 copy.14
  216.5 1.0 fusion.29
  217.4 1.0 slice_convert_fusion
  218.5 0.1 convert_element_type.98
  218.5 0.2 convert_reduce_fusion
  218.7 0.6 reduce_max.9
  220.0 0.1 select_reduce_fusion.4
  220.1 0.5 fusion.8
  220.6 30.7 %conditional.1 = (bf16[4008,4096]{1,0:T(8,128)(2,1)}) conditional(s32[]{:T(128)} %convert_element_type.100, (s32[32,32]{1,0:T(8,128)S(1)}, f32[32,32]{1,0:T(8,128)S(1)}, bf16[1024,4096]{1,0:T(8,128)(2,1)}) %tuple.27, (s32[1,3]{1,0:T(1,128)S(1)}, s32[1024,3]{0,1:T(4,128)S(1)}, pred[1024,3]{0,1:T(4,128)(4,1)S(1)}, s32[32,32]{1,0:T(8,128)S(1)}, ...), branch_computations={%region_10.11_spmd, %region_11.15_spmd} | conditional | flops 33654644736 | bytes 53934480 | solution.py:223
  220.7 0.1 select_reduce_fusion.2
  220.8 0.1 broadcast_in_dim.56
  220.9 0.4 select_reduce_fusion
  221.3 12.0 %multiply_convert_fusion.2 = bf16[768,4096]{1,0:T(8,128)(2,1)} fusion(bf16[1024,4096]{1,0:T(8,128)(2,1)} %get-tuple-element.52, f32[768]{0:T(1024)S(1)} %select_reduce_fusion, s32[1024]{0:T(1024)S(1)} %broadcast_add_fusion.2), kind=kOutput, calls=%fused_computation.6 | convolution fusion | flops 6449528832 | bytes 14687232 | tf_op jit(solution)/shard_map/cond/branch_1_fun/dot_general | solution.py:211
  233.3 0.1 add.108
  233.3 0.4 select_reduce_fusion.1
  233.8 0.1 iota_add_fusion
  233.8 17.4 %convolution_convert_fusion.1 = bf16[3,1336,4096]{2,1,0:T(8,128)(2,1)} fusion(bf16[3,256,4096]{2,1,0:T(8,128)(2,1)} %bitcast.49, s32[3,1336]{1,0:T(4,128)S(1)} %iota_add_fusion, s32[3,256]{1,0:T(4,128)S(1)} %sub.36), kind=kOutput, calls=%fused_computation.5 | convolution fusion | flops 8422828032 | bytes 39144096 | tf_op jit(solution)/shard_map/cond/branch_1_fun/dot_general | solution.py:215
  (17 shorter events, 0.1 us)
Async XLA Ops:
  15.8 198.6 %copy-start = (s32[64]{0:T(128)S(1)}, s32[64]{0:T(128)}, u32[]{:S(2)}) copy-start(s32[64]{0:T(128)} %param.18) | copy-start | bytes 772
  15.8 198.6 %copy-start.1 = (s32[64]{0:T(128)S(1)}, s32[64]{0:T(128)}, u32[]{:S(2)}) copy-start(s32[64]{0:T(128)} %param.17) | copy-start | bytes 772
